TPU v7x, 32 devices: a whole 2x2x4 slice. The times are simulated.
32 devices in a mesh: row: 4 (over y, x), col: 8 (over z, core).
Axes of the slice: x: 2, y: 2, z: 4, core: 2. Of those that a mesh axis runs over, the one named last changes fastest.
Arguments:
- inverse_state: float32 [8, 1024, 4, 2048], P(None, 'row', None, 'col')
- row_seeds: int32 [2, 8, 1024], P(None, None, 'row'), may hold values from 0 to 31
- col_seeds: int32 [2, 4, 2048], P(None, None, 'col'), may hold values from 0 to 31
Outputs:
- inverse: float32 [8, 1024, 4, 2048], P(None, 'row', None, 'col')
All inputs are finite; a program needn't handle non-finite values.
Results may differ from a plain program's by a relative error of at most 0.0002.
Values sent between devices are 32-bit elements; how exact they have to be, the bound alone decides.
A program may use at most 64 MiB of HBM per device.

v0:
```python
import jax
import jax.numpy as jnp
from jax import lax
from jax.sharding import PartitionSpec as P

STEPS = 2


root_half = 0.7071067811865476


def broadcast(x, axis, root):
    mine = lax.axis_index(axis) == root
    return lax.psum(jnp.where(mine, x, jnp.zeros_like(x)), axis)


def swapped(block, axis, bit):
    count = lax.axis_size(axis)
    route = []
    for low in range(count):
        high = low | 1 << bit
        if high != low and high < count:
            route += [(low, high), (high, low)]
    return lax.ppermute(block, axis, route)


def seed_values(seeds):
    return (2.0 * seeds.astype(jnp.float32) - 31.0) / 16.0


def row_level(matrix, scales, groups):
    count = matrix.shape[0]
    half = count // (2 * groups)
    shaped = matrix.reshape((groups, 2, half) + matrix.shape[1:])
    factor = scales.reshape((groups, 2, half, scales.shape[1]) + (1,) * (matrix.ndim - 2))
    upper = factor[:, 0] * shaped[:, 0]
    lower = factor[:, 1] * shaped[:, 1]
    return (jnp.stack([upper + lower, upper - lower], axis=1) * root_half).reshape(matrix.shape)


def row_butterfly(matrix, seeds):
    scales = seed_values(seeds)
    return row_level(row_level(matrix, scales[0], 1), scales[1], 2)


def col_level(matrix, scales, groups, mover, col_index, span):
    if mover is None:
        count = matrix.shape[1]
        half = count // (2 * groups)
        shaped = matrix.reshape(matrix.shape[0], groups, 2, half, matrix.shape[2])
        factor = scales.reshape(groups, 2, half, scales.shape[1])
        upper = factor[:, 0] * shaped[:, :, 0]
        lower = factor[:, 1] * shaped[:, :, 1]
        return (jnp.stack([upper + lower, upper - lower], axis=2) * root_half).reshape(matrix.shape)
    own_part = scales * matrix
    partner = mover(own_part)
    on_top = col_index // span % 2 == 0
    return jnp.where(on_top, own_part + partner, partner - own_part) * root_half


def col_butterfly(matrix, seeds, first_mover, second_mover):
    scales = seed_values(seeds)
    col_count = lax.axis_size("col")
    col_index = lax.axis_index("col")
    blocks_all = matrix.shape[1] * col_count
    span_one = blocks_all // 2
    span_two = blocks_all // 4
    first_use = None if span_one % col_count == 0 else first_mover
    second_use = None if span_two % col_count == 0 else second_mover
    matrix = col_level(matrix, scales[0], 1, first_use, col_index, span_one)
    return col_level(matrix, scales[1], 2, second_use, col_index, span_two)


def solve_block(pivot, rows_given):
    gram = jnp.dot(
        pivot.T, pivot, precision=lax.Precision.HIGHEST, preferred_element_type=jnp.float32
    )
    factor = jnp.linalg.cholesky(gram)
    right_side = jnp.dot(
        pivot.T, rows_given, precision=lax.Precision.HIGHEST, preferred_element_type=jnp.float32
    )
    middle = lax.linalg.triangular_solve(factor, right_side, left_side=True, lower=True)
    return lax.linalg.triangular_solve(factor, middle, left_side=True, lower=True, transpose_a=True)


def pivot_pieces(state, step):
    row_blocks = state.shape[0]
    block = state.shape[1]
    col_blocks = state.shape[2]
    row_count = lax.axis_size("row")
    col_count = lax.axis_size("col")
    target = row_blocks * row_count - STEPS + step
    row_root = target % row_count
    row_local = target // row_count
    col_root = target % col_count
    col_local = target // col_count
    on_row = lax.axis_index("row") == row_root
    on_col = lax.axis_index("col") == col_root
    identity = jnp.eye(block, dtype=jnp.float32)
    column = broadcast(state[:, :, col_local, :], "col", col_root)
    pivot = jnp.where(on_row, column[row_local], identity)
    left_part = column.at[row_local].set(jnp.where(on_row, pivot - identity, column[row_local]))
    last_column = jnp.where(on_col, 0.0, state[:, :, col_local, :])
    last_column = last_column.at[row_local].set(
        jnp.where(on_row & on_col, identity, last_column[row_local])
    )
    shifted = state.at[:, :, col_local, :].set(last_column)
    pivot_rows = shifted[row_local].reshape(block, col_blocks * block)
    rows_there, pivot_there = (
        broadcast(pivot_rows, "row", row_root),
        broadcast(pivot, "row", row_root),
    )
    right_part = solve_block(pivot_there, rows_there)
    return (shifted, left_part, right_part)


def apply_update(shifted, left_part, right_part):
    row_blocks, block, col_blocks, _ = shifted.shape
    flat_left = left_part.reshape(row_blocks * block, block)
    update = shifted.reshape(row_blocks * block, col_blocks * block) - jnp.dot(
        flat_left, right_part, precision=lax.Precision.HIGHEST, preferred_element_type=jnp.float32
    )
    return update.reshape(shifted.shape)


def per_device(inverse_state, row_seeds, col_seeds):
    row_blocks = inverse_state.shape[0]
    block = inverse_state.shape[1]
    col_blocks = inverse_state.shape[2]
    col_count = lax.axis_size("col")
    state = inverse_state
    shifted, left_part, right_part = pivot_pieces(state, 0)
    state = apply_update(shifted, left_part, right_part)
    shifted, left_part, right_part = pivot_pieces(state, STEPS - 1)
    blocks_all = col_blocks * col_count
    bit_one = (blocks_all // 2).bit_length() - 1
    bit_two = (blocks_all // 4).bit_length() - 1
    moved = row_butterfly(shifted, row_seeds)
    moved = col_butterfly(
        moved.reshape(row_blocks * block, col_blocks, block),
        col_seeds,
        lambda values: swapped(values, "col", bit_one),
        lambda values: swapped(values, "col", bit_two),
    )
    left_moved = row_butterfly(left_part, row_seeds).reshape(row_blocks * block, block)
    right_moved = col_butterfly(
        right_part.reshape(block, col_blocks, block),
        col_seeds,
        lambda values: swapped(values, "col", bit_one),
        lambda values: swapped(values, "col", bit_two),
    )
    product = jnp.dot(
        left_moved,
        right_moved.reshape(block, col_blocks * block),
        precision=lax.Precision.HIGHEST,
        preferred_element_type=jnp.float32,
    )
    result = moved - product.reshape(moved.shape)
    return result.reshape(inverse_state.shape)


def solution(mesh):
    placed = (P(None, "row", None, "col"), P(None, None, "row"), P(None, None, "col"))
    return jax.shard_map(
        per_device,
        mesh=mesh,
        in_specs=placed,
        out_specs=P(None, "row", None, "col"),
        check_vma=False,
    )
```

profile of v0, /device:TPU:0, one launch (start us, length us, event | category | flops | bytes accessed | tf_op | source)
XLA Modules:
  0.0 524.7 jit_solution(7826115998392346241)
XLA Ops:
  6.5 8.2 %copy.81 = f32[8,256,4,256]{3,2,1,0:T(4,128)} copy(f32[8,256,4,256]{3,2,1,0:T(4,128)} %param.20) | data formatting | bytes 16777216
  14.8 6.9 %slice.325 = f32[8,256,1,256]{3,2,1,0:T(1,128)} slice(f32[8,256,4,256]{3,2,1,0:T(4,128)} %copy.81), slice={[0:8], [0:256], [3:4], [0:256]} | slice | bytes 4194304 | tf_op jit(solution)/shard_map/slice | solution.py:103
  21.6 3.4 select_bitcast_fusion.1
  25.1 3.5 copy.20
  28.6 45.9 %scatter.21 = f32[8,256,4,256]{3,2,1,0:T(4,128)} dynamic-update-slice(f32[8,256,4,256]{3,2,1,0:T(4,128)} %copy.81, f32[8,256,1,256]{3,2,1,0:T(1,128)} %copy.20, s32[]{:T(128)} %copy.82, s32[]{:T(128)} %copy.82, s32[]{:T(128)} %constant.242.clone.1, s32[]{:T(128)} %copy.82) | dynamic-update-slice | bytes 4194308 | tf_op jit(solution)/shard_map/scatter | solution.py:107
  77.4 8.8 %copy.38 = f32[256,8,4,256]{3,1,2,0:T(8,128)} copy(f32[256,8,4,256]{3,2,1,0:T(4,128)} %bitcast.166) | data formatting | bytes 16777216
  86.2 6.7 %all-reduce.8.cloned.1.call-done = f32[8,256,256]{2,1,0:T(8,128)} async-done(((f32[8,256,256]{2,1,0:T(8,128)}), f32[8,256,256]{2,1,0:T(8,128)}) %all-reduce.8.cloned.1.call-update) | async-done | bytes 2097168 | tf_op jit(solution)/shard_map/psum | solution.py:14
  96.7 55.4 %all-reduce.14.cloned.1.call-done = (f32[256,256]{1,0:T(8,128)}, f32[256,1024]{1,0:T(8,128)}) async-done(((f32[256,256]{1,0:T(8,128)}, f32[256,1024]{1,0:T(8,128)}), (f32[256,256]{1,0:T(8,128)}, f32[256,1024]{1,0:T(8,128)})) %all-reduce.14.cloned.1.call-update) | async-done | bytes 1310736 | tf_op jit(solution)/shard_map/psum | solution.py:14
  152.1 1.7 fusion.51
  154.0 11.7 %cholesky.130 = f32[128,128]{1,0:T(8,128)S(1)} custom-call(f32[128,128]{1,0:T(8,128)S(1)} %cholesky.194), custom_call_target="Cholesky" | custom-call | tf_op jit(solution)/shard_map/jit(cholesky)/cholesky | solution.py:78
  165.8 9.8 %custom-call.17 = f32[1,128,128]{1,2,0:T(8,128)S(1)} custom-call(f32[1,128,128]{2,1,0:T(8,128)S(1)} %get-tuple-element.163), custom_call_target="InvertDiagBlocksLowerTriangular" | custom-call | tf_op jit(solution)/shard_map/jit(cholesky)/cholesky | solution.py:78
  176.1 11.7 %cholesky.147 = f32[128,128]{1,0:T(8,128)S(1)} custom-call(f32[128,128]{1,0:T(8,128)S(1)} %convolution_subtract_fusion.6), custom_call_target="Cholesky" | custom-call | tf_op jit(solution)/shard_map/jit(cholesky)/cholesky | solution.py:78
  190.1 4.3 while.14
  194.4 19.7 %custom-call.19 = f32[2,128,128]{1,2,0:T(8,128)S(1)} custom-call(f32[2,128,128]{2,1,0:T(8,128)S(1)} %get-tuple-element.109), custom_call_target="InvertDiagBlocksLowerTriangular" | custom-call | tf_op jit(solution)/shard_map/triangular_solve/custom-call.4 | solution.py:83
  218.8 11.0 %convolution_subtract_fusion = f32[2048,1024]{1,0:T(8,128)} fusion(f32[2048,1024]{1,0:T(8,128)} %bitcast.169, f32[2048,256]{1,0:T(8,128)S(1)} %bitcast.182, f32[128,1024]{1,0:T(8,128)S(1)} %fusion.37, f32[128,1024]{1,0:T(8,128)S(1)} %fusion.35), kind=kOutput, calls=%fused_computation.9 | convolution fusion | flops 6444810240 | bytes 19922944 | tf_op jit(solution)/shard_map/dot_general | solution.py:120
  229.8 11.0 %reshape.530 = f32[8,256,4,256]{3,2,1,0:T(4,128)} reshape(f32[2048,1024]{1,0:T(8,128)} %convolution_subtract_fusion) | data formatting | bytes 16777216 | tf_op jit(solution)/shard_map/reshape | solution.py:123
  240.8 5.5 %slice.429 = f32[8,256,1,256]{3,2,1,0:T(1,128)S(1)} slice(f32[8,256,4,256]{3,2,1,0:T(4,128)} %reshape.530), slice={[0:8], [0:256], [3:4], [0:256]} | slice | bytes 4194304 | tf_op jit(solution)/shard_map/slice | solution.py:103
  248.1 2.2 copy.23
  250.3 45.7 %scatter.26 = f32[8,256,4,256]{3,2,1,0:T(4,128)} dynamic-update-slice(f32[8,256,4,256]{3,2,1,0:T(4,128)} %reshape.530, f32[8,256,1,256]{3,2,1,0:T(1,128)S(1)} %copy.23, s32[]{:T(128)} %copy.82, s32[]{:T(128)} %copy.82, s32[]{:T(128)} %constant.242.clone.1, s32[]{:T(128)} %copy.82) | dynamic-update-slice | bytes 4194308 | tf_op jit(solution)/shard_map/scatter | solution.py:107
  298.7 6.1 %fusion.5 = (f32[1,1,4,256,4,256]{5,4,3,2,1,0:T(4,128)S(1)}, f32[1,1,4,256,4,256]{5,4,3,2,1,0:T(4,128)S(1)}) fusion(f32[1,2,4,256,4,256]{5,4,3,2,1,0:T(4,128)} %bitcast.167, f32[4,256]{1,0:T(4,128)S(1)} %get-tuple-element.175, f32[4,256]{1,0:T(4,128)S(1)} %get-tuple-element.174), kind=kLoop, calls=%fused_computation.25 | loop fusion | flops 4194304 | bytes 16785408 | tf_op jit(solution)/shard_map/add | solution.py:38
  311.6 4.0 fusion.3
  315.6 48.2 %all-reduce.10.cloned.1.call-done = f32[8,256,256]{2,1,0:T(8,128)} async-done(((f32[8,256,256]{2,1,0:T(8,128)}), f32[8,256,256]{2,1,0:T(8,128)}) %all-reduce.10.cloned.1.call-update) | async-done | bytes 2097168 | tf_op jit(solution)/shard_map/psum | solution.py:14
  365.6 7.9 %maximum_multiply_fusion.3 = f32[2048,2,2,1,256]{4,0,2,1,3:T(8,128)} fusion(f32[2048,2,1,1,256]{4,0,2,1,3:T(8,128)} %get-tuple-element.141, f32[2048,2,1,1,256]{4,0,2,1,3:T(8,128)} %get-tuple-element.140), kind=kLoop, calls=%fused_computation.7 | loop fusion | flops 4194304 | bytes 16777216 | tf_op jit(solution)/shard_map/mul | solution.py:54
  374.7 48.1 %all-reduce.12.cloned.1.call-done = (f32[256,256]{1,0:T(8,128)}, f32[256,1024]{1,0:T(8,128)}) async-done(((f32[256,256]{1,0:T(8,128)}, f32[256,1024]{1,0:T(8,128)}), (f32[256,256]{1,0:T(8,128)}, f32[256,1024]{1,0:T(8,128)})) %all-reduce.12.cloned.1.call-update) | async-done | bytes 1310736 | tf_op jit(solution)/shard_map/psum | solution.py:14
  424.7 11.7 %cholesky.164 = f32[128,128]{1,0:T(8,128)S(1)} custom-call(f32[128,128]{1,0:T(8,128)S(1)} %cholesky.197), custom_call_target="Cholesky" | custom-call | tf_op jit(solution)/shard_map/jit(cholesky)/cholesky | solution.py:78
  436.5 9.8 %custom-call.20 = f32[1,128,128]{1,2,0:T(8,128)S(1)} custom-call(f32[1,128,128]{2,1,0:T(8,128)S(1)} %get-tuple-element.159), custom_call_target="InvertDiagBlocksLowerTriangular" | custom-call | tf_op jit(solution)/shard_map/jit(cholesky)/cholesky | solution.py:78
  446.8 11.9 %cholesky.181 = f32[128,128]{1,0:T(8,128)S(1)} custom-call(f32[128,128]{1,0:T(8,128)S(1)} %convolution_subtract_fusion.5), custom_call_target="Cholesky" | custom-call | tf_op jit(solution)/shard_map/jit(cholesky)/cholesky | solution.py:78
  461.4 3.9 while.15
  465.3 19.7 %custom-call.22 = f32[2,128,128]{1,2,0:T(8,128)S(1)} custom-call(f32[2,128,128]{2,1,0:T(8,128)S(1)} %get-tuple-element.111), custom_call_target="InvertDiagBlocksLowerTriangular" | custom-call | tf_op jit(solution)/shard_map/triangular_solve/custom-call.4 | solution.py:83
  485.0 2.3 fusion.54
  494.2 11.3 %bitcast_subtract_fusion = f32[2048,4,256]{2,0,1:T(8,128)} fusion(f32[2048,2,2,1,256]{4,0,2,1,3:T(8,128)} %maximum_multiply_fusion.3, f32[2048,256,1]{1,0,2:T(8,128)S(1)} %bitcast.173, f32[4,256,256]{2,1,0:T(8,128)S(1)} %bitcast.174), kind=kOutput, calls=%fused_computation.8 | convolution fusion | flops 6444548096 | bytes 19922944 | tf_op jit(solution)/shard_map/dot_general | solution.py:152
  505.5 12.2 %copy.32 = f32[8,256,4,256]{3,2,1,0:T(4,128)} copy(f32[8,256,4,256]{3,1,0,2:T(8,128)} %bitcast.170) | data formatting | bytes 16777216 | tf_op jit(solution)/shard_map/reshape | solution.py:159
  (118 shorter events, 45.6 us)
Async XLA Ops:
  6.5 86.4 %all-reduce.8.cloned.1.call-start = ((), (), s32[]{:S(2)}) async-start(), calls=%async_computation | async-start | bytes 4194304 | tf_op jit(solution)/shard_map/psum | solution.py:14
  25.0 127.1 %all-reduce.14.cloned.1.call-start = ((), (), s32[]{:S(2)}) async-start(), calls=%async_computation.3 | async-start | bytes 2621440 | tf_op jit(solution)/shard_map/psum | solution.py:14
  28.6 47.4 %copy-start.5 = (s32[2,8,256]{2,1,0:T(8,128)S(1)}, s32[2,8,256]{2,1,0:T(8,128)}, u32[]{:S(2)}) copy-start(s32[2,8,256]{2,1,0:T(8,128)} %param.21) | copy-start | bytes 49156
  77.4 8.8 %copy-start.6 = (s32[2,4,256]{2,1,0:T(4,128)S(1)}, s32[2,4,256]{2,1,0:T(4,128)}, u32[]{:S(2)}) copy-start(s32[2,4,256]{2,1,0:T(4,128)} %param.22) | copy-start | bytes 24580
  94.7 269.2 %all-reduce.10.cloned.1.call-start = ((), (), s32[]{:S(2)}) async-start(), calls=%async_computation.1 | async-start | bytes 4194304 | tf_op jit(solution)/shard_map/psum | solution.py:14
  152.1 62.0 %copy-start.3 = (f32[256,256]{1,0:T(8,128)S(1)}, f32[256,256]{1,0:T(8,128)}, u32[]{:S(2)}) copy-start(f32[256,256]{1,0:T(8,128)} %get-tuple-element.130) | copy-start | bytes 786436
  152.1 62.0 %copy-start.4 = (f32[256,1024]{1,0:T(8,128)S(1)}, f32[256,1024]{1,0:T(8,128)}, u32[]{:S(2)}) copy-start(f32[256,1024]{1,0:T(8,128)} %get-tuple-element.131) | copy-start | bytes 3145732
  215.1 3.7 copy-start
  298.6 124.2 %all-reduce.12.cloned.1.call-start = ((), (), s32[]{:S(2)}) async-start(), calls=%async_computation.2 | async-start | bytes 2621440 | tf_op jit(solution)/shard_map/psum | solution.py:14
  365.6 8.0 %copy-start.1 = (f32[8,256,256]{2,1,0:T(8,128)S(1)}, f32[8,256,256]{2,1,0:T(8,128)}, u32[]{:S(2)}) copy-start(f32[8,256,256]{2,1,0:T(8,128)} %all-reduce.10.cloned.1.call-done) | copy-start | bytes 6291460
  422.8 62.1 %copy-start.2 = (f32[256,256]{1,0:T(8,128)S(1)}, f32[256,256]{1,0:T(8,128)}, u32[]{:S(2)}) copy-start(f32[256,256]{1,0:T(8,128)} %get-tuple-element.128) | copy-start | bytes 786436
Sparse Core Ops, SparseCore 0:
  25.1 67.7 all-reduce.7
  96.1 56.0 all-reduce.13
  298.7 65.0 all-reduce.9
  366.8 55.9 all-reduce.11
where the time goes:
time: 535 us; the launch traced here: 525 us
  local copies, waits for them, and re-layouts  164 us (31%)
  waiting for transfers between devices  159 us (30%)
  other arithmetic  148 us (28%)
  matrix products  37.3 us (7%)
  between operations  16.8 us (3%)
    psum x4, waiting for transfers between devices, broadcast(): return lax.psum(jnp.where(mine, x, jnp.zeros_like(x)), axis)  159 us
    scatter x2, local copies, waits for them, and re-layouts, pivot_pieces(): shifted = state.at[:, :, col_local, :].set(last_column)  91.6 us
    another operation x13, other arithmetic, solve_block(): factor = jnp.linalg.cholesky(gram)  68.9 us
    another operation x6, other arithmetic, solve_block(): lax.linalg.triangular_solve(factor, middle, left_side=True, lower=True, t...  40.5 us
    unnamed x18, local copies, waits for them, and re-layouts  19.4 us
    slice x2, local copies, waits for them, and re-layouts, pivot_pieces(): last_column = jnp.where(on_col, 0.0, state[:, :, col_local, :])  12.4 us
    reshape x1, local copies, waits for them, and re-layouts, per_device(): return result.reshape(inverse_state.shape)  12.2 us
    select_n x6, other arithmetic, broadcast(): return lax.psum(jnp.where(mine, x, jnp.zeros_like(x)), axis)  11.4 us
  transfers between devices with their start and end apart: 4, of which 4 were waited for; matrix products, arithmetic and copies ran while one was open for 17% of the time, Pallas kernels for 0%

commit v1 on v0

v1 whole, which is shorter than its diff:
```python
import functools

import jax
import jax.numpy as jnp
from jax import lax
from jax.experimental import pallas as pl
from jax.experimental.pallas import tpu as pltpu
from jax.sharding import PartitionSpec as P

STEPS = 2
LANES = 128
root_half = 0.7071067811865476
HIGHEST = lax.Precision.HIGHEST
VMEM_BYTES = 60 * 1024 * 1024


def swapped(block, axis, bit):
    count = lax.axis_size(axis)
    route = []
    for low in range(count):
        high = low | 1 << bit
        if high != low and high < count:
            route += [(low, high), (high, low)]
    return lax.ppermute(block, axis, route)


def seed_values(seeds):
    return (2.0 * seeds.astype(jnp.float32) - 31.0) / 16.0


def col_level(matrix, scales, groups, mover, col_index, span):
    if mover is None:
        count = matrix.shape[1]
        half = count // (2 * groups)
        shaped = matrix.reshape(matrix.shape[0], groups, 2, half, matrix.shape[2])
        factor = scales.reshape(groups, 2, half, scales.shape[1])
        upper = factor[:, 0] * shaped[:, :, 0]
        lower = factor[:, 1] * shaped[:, :, 1]
        return (jnp.stack([upper + lower, upper - lower], axis=2) * root_half).reshape(matrix.shape)
    own_part = scales * matrix
    partner = mover(own_part)
    on_top = col_index // span % 2 == 0
    return jnp.where(on_top, own_part + partner, partner - own_part) * root_half


def col_butterfly(matrix, seeds):
    scales = seed_values(seeds)
    col_count = lax.axis_size("col")
    col_index = lax.axis_index("col")
    blocks_all = matrix.shape[1] * col_count
    for level, groups in ((0, 1), (1, 2)):
        span = blocks_all // (2 * groups)
        bit = span.bit_length() - 1
        mover = None if span % col_count == 0 else lambda values: swapped(values, "col", bit)
        matrix = col_level(matrix, scales[level], groups, mover, col_index, span)
    return matrix


def levels(parts, first, second):
    count = len(parts)
    for scales, groups in ((first, 1), (second, 2)):
        half = count // (2 * groups)
        done = list(parts)
        for group in range(groups):
            for at in range(half):
                top = group * 2 * half + at
                low = top + half
                upper = scales[top] * parts[top]
                lower = scales[low] * parts[low]
                done[top] = upper + lower
                done[low] = upper - lower
        parts = done
    return parts


def split(x):
    high = x.astype(jnp.bfloat16)
    return high, (x - high.astype(jnp.float32)).astype(jnp.bfloat16)


def dot_f32(a, b):
    return jnp.dot(a, b, precision=HIGHEST, preferred_element_type=jnp.float32)


def dot_split(a, b):
    a_high, a_low = split(a)
    b_high, b_low = split(b)
    dot = functools.partial(jnp.dot, preferred_element_type=jnp.float32)
    return dot(a_high, b_high) + dot(a_high, b_low) + dot(a_low, b_high)


def eye_of(rows, columns, row_start=0, column_start=0):
    at_row = lax.broadcasted_iota(jnp.int32, (rows, columns), 0) + row_start
    at_column = lax.broadcasted_iota(jnp.int32, (rows, columns), 1) + column_start
    return jnp.where(at_row == at_column, 1.0, 0.0).astype(jnp.float32)


def extract_kernel(row_blocks, col_blocks, block, x_ref, c_ref, r_ref):
    stride = col_blocks * (block // LANES)

    def piece(b, h):
        return x_ref[pl.ds(h * col_blocks + b, block, stride=stride), :]

    for h in range(block // LANES):
        c_ref[0, :, h * LANES:(h + 1) * LANES] = piece(col_blocks - 1, h)

    @pl.when(pl.program_id(0) == row_blocks - 1)
    def _():
        for b in range(col_blocks):
            for h in range(block // LANES):
                start = b * block + h * LANES
                r_ref[:, start:start + LANES] = piece(b, h)


def spread_kernel(
    chunk_count, piece_count, col_count, row_count,
    c_ref, r_ref, cpan, rpan, ppan,
    c_down, c_down_in, c_mate, c_mate_in,
    r_down, r_down_in, r_mate, r_mate_in,
    p_down, p_down_in, p_mate, p_mate_in, p_core, p_core_in, local,
):
    row_blocks, block, _ = c_ref.shape
    col, row = lax.axis_index("col"), lax.axis_index("row")
    k, j = lax.rem(col, 2), lax.rem(row, 2)
    col_mate, row_mate = col + 1 - 2 * k, row + 1 - 2 * j
    col_root, row_root = col >= col_count - 2, row >= row_count - 2
    col_has, row_has = col >= 2, row >= 2
    col_low, row_low = jnp.maximum(col - 2, 0), jnp.maximum(row - 2, 0)
    col_up = jnp.minimum(col + 2, col_count - 1)
    row_up = jnp.minimum(row + 2, row_count - 1)

    barrier = pltpu.get_barrier_semaphore()

    def greet(axis, target):
        pl.semaphore_signal(
            barrier, inc=1, device_id={axis: target}, device_id_type=pl.DeviceIdType.MESH
        )

    greet("col", col_mate)
    greet("row", row_mate)
    pl.when(col_has)(lambda: greet("col", col_low))
    pl.when(row_has)(lambda: greet("row", row_low))
    pl.when(jnp.logical_not(col_root))(lambda: greet("col", col_up))
    pl.when(jnp.logical_not(row_root))(lambda: greet("row", row_up))
    peers = 4 - col_root.astype(jnp.int32) - row_root.astype(jnp.int32)
    peers = peers + col_has.astype(jnp.int32) + row_has.astype(jnp.int32)
    pl.semaphore_wait(barrier, peers)

    def remote(src, dst, send, receive, axis, target):
        return pltpu.make_async_remote_copy(
            src_ref=src, dst_ref=dst, send_sem=send, recv_sem=receive,
            device_id={axis: target}, device_id_type=pl.DeviceIdType.MESH,
        )

    own_c = pltpu.make_async_copy(c_ref, cpan.at[k], local.at[0])
    own_r = pltpu.make_async_copy(r_ref, rpan.at[j], local.at[1])
    own_p = pltpu.make_async_copy(cpan.at[k, row_blocks - 1], ppan.at[k, j], local.at[2])
    pl.when(col_root)(own_c.start)
    pl.when(row_root)(own_r.start)
    pl.when(col_root)(own_c.wait)
    pl.when(row_root)(own_r.wait)

    per_block = chunk_count // row_blocks
    rows_each = block // per_block

    def c_at(side, index):
        a = row_blocks - 1 - index // per_block
        return cpan.at[side, a, pl.ds(index % per_block * rows_each, rows_each), :]

    def c_step(index):
        down = remote(c_at(k, index), c_at(k, index), c_down.at[index], c_down_in.at[index], "col", col_low)
        mate = remote(c_at(k, index), c_at(k, index), c_mate.at[index], c_mate_in.at[index], "col", col_mate)
        pl.when(jnp.logical_not(col_root))(down.wait_recv)
        pl.when(col_has)(down.start)
        mate.start()
        return down, mate

    piece_rows = block // piece_count

    def r_at(side, index):
        return rpan.at[side, pl.ds(index * piece_rows, piece_rows), :]

    def r_step(index):
        down = remote(r_at(j, index), r_at(j, index), r_down.at[index], r_down_in.at[index], "row", row_low)
        mate = remote(r_at(j, index), r_at(j, index), r_mate.at[index], r_mate_in.at[index], "row", row_mate)
        pl.when(jnp.logical_not(row_root))(down.wait_recv)
        pl.when(row_has)(down.start)
        mate.start()
        return down, mate

    c_copies, r_copies = [], []
    for index in range(per_block):
        c_copies.append(c_step(index))

    p_low = remote(ppan.at[k, j], ppan.at[k, j], p_down, p_down_in, "row", row_low)
    p_side = remote(ppan.at[k, j], ppan.at[k, j], p_mate, p_mate_in, "row", row_mate)
    p_over = remote(ppan.at[k], ppan.at[k], p_core, p_core_in, "col", col_mate)

    pl.when(row_root)(own_p.start)
    pl.when(row_root)(own_p.wait)
    pl.when(jnp.logical_not(row_root))(p_low.wait_recv)
    pl.when(row_has)(p_low.start)
    p_side.start()

    done = 0
    for index in range(per_block, chunk_count):
        c_copies.append(c_step(index))
        wanted = min(piece_count, index - per_block + 1)
        while done < wanted:
            r_copies.append(r_step(done))
            done += 1
    while done < piece_count:
        r_copies.append(r_step(done))
        done += 1
    p_side.wait_recv()
    p_over.start()

    for down, mate in c_copies:
        mate.wait_recv()
        mate.wait_send()
        pl.when(col_has)(down.wait_send)
    for down, mate in r_copies:
        mate.wait_recv()
        mate.wait_send()
        pl.when(row_has)(down.wait_send)
    p_side.wait_send()
    pl.when(row_has)(p_low.wait_send)
    p_over.wait_recv()
    p_over.wait_send()


def inverse_of(matrix, cap=60):
    size = matrix.shape[0]
    identity = eye_of(size, size)
    matrix_t = matrix.T
    gram = dot_split(matrix_t, matrix)
    bound = jnp.max(jnp.sum(jnp.abs(gram), axis=0, keepdims=True))
    guess = matrix_t * (1.8 / bound)

    def going(carry):
        count, _, worst, before = carry
        return jnp.logical_and(
            count < cap,
            jnp.logical_or(worst > 1e-2, jnp.logical_and(worst > 1e-6, worst < 0.5 * before)),
        )

    def body(carry):
        count, x, worst, _ = carry
        error = identity - dot_f32(matrix, x)
        x = x + dot_split(x, error)
        return count + 1, x, jnp.max(jnp.abs(error)), worst

    start = (jnp.int32(0), guess, jnp.float32(1e30), jnp.float32(1e30))
    return lax.while_loop(going, body, start)[1]


def solve_kernel(col_blocks, block, local_cols, flags, p_ref, r_ref, d_ref, high_ref, low_ref):
    a11, a21 = p_ref[0, 0], p_ref[0, 1]
    a12, a22 = p_ref[1, 0], p_ref[1, 1]
    last = (col_blocks - 1) * block
    identity = eye_of(block, block)
    for step in range(STEPS):
        here = jnp.where(flags[1] == step, identity, jnp.zeros_like(identity))

        @pl.when(flags[0] == 1)
        def _():
            r_ref[step, :, last:] = here

    first_inverse = inverse_of(a11)
    low_left = dot_f32(a21, first_inverse)
    second_inverse = inverse_of(a22 - dot_f32(low_left, a12))
    right = dot_f32(second_inverse, r_ref[1] - dot_f32(low_left, r_ref[0]))
    left = dot_f32(first_inverse, r_ref[0] - dot_f32(a12, right))
    for step, value in ((0, left), (1, right)):
        parts = [value[:, b * block:(b + 1) * block] for b in range(col_blocks)]
        if local_cols:
            scales = [
                [d_ref[level:level + 1, b * block:(b + 1) * block] for b in range(col_blocks)]
                for level in range(2)
            ]
            parts = levels(parts, *scales)
        for b, part in enumerate(parts):
            high, low = split(part)
            high_ref[step * block:(step + 1) * block, b * block:(b + 1) * block] = high
            low_ref[step * block:(step + 1) * block, b * block:(b + 1) * block] = low


def final_kernel(
    row_blocks, col_blocks, block, tile, local_cols, flags,
    x_ref, c_ref, rd_ref, cd_ref, high_ref, low_ref, out_ref, left_high, left_low, product,
):
    halves = block // LANES
    stride = col_blocks * halves
    start = pl.program_id(0) * tile
    row_scales = [
        [rd_ref[:, level * row_blocks + a:level * row_blocks + a + 1] for a in range(row_blocks)]
        for level in range(2)
    ]
    for step in range(STEPS):
        for h in range(halves):
            lanes = pl.ds(h * LANES, LANES)
            parts = [c_ref[step, a, :, lanes] for a in range(row_blocks)]
            parts[-1] = parts[-1] - jnp.where(
                flags[2] == step, eye_of(tile, LANES, start, h * LANES), 0.0
            )
            for a, part in enumerate(levels(parts, *row_scales)):
                high, low = split(part)
                place = (pl.ds(a * tile, tile), pl.ds(step * block + h * LANES, LANES))
                left_high[place] = high
                left_low[place] = low
    dot = functools.partial(jnp.dot, preferred_element_type=jnp.float32)
    for b in range(col_blocks):
        at = pl.ds(b * block, block)
        product[:, at] = (
            dot(left_high[...], high_ref[:, at])
            + dot(left_high[...], low_ref[:, at])
            + dot(left_low[...], high_ref[:, at])
        )
    for h in range(halves):
        columns = []
        for b in range(col_blocks):
            at = pl.ds(h * col_blocks + b, tile, stride=stride)
            parts = [x_ref[a, at, :] for a in range(row_blocks)]
            if b == col_blocks - 1:
                parts = [jnp.where(flags[0] == 1, 0.0, part) for part in parts]
                parts[-1] = parts[-1] + jnp.where(
                    flags[3] == 1, eye_of(tile, LANES, start, h * LANES), 0.0
                )
            columns.append(levels(parts, *row_scales))
        for a in range(row_blocks):
            parts = [columns[b][a] for b in range(col_blocks)]
            if local_cols:
                scales = [
                    [
                        cd_ref[level:level + 1, b * block + h * LANES:b * block + (h + 1) * LANES]
                        for b in range(col_blocks)
                    ]
                    for level in range(2)
                ]
                parts = levels(parts, *scales)
            for b in range(col_blocks):
                at = pl.ds(h * col_blocks + b, tile, stride=stride)
                spot = b * block + h * LANES
                out_ref[a, at, :] = parts[b] - product[a * tile:(a + 1) * tile, spot:spot + LANES]


def per_device(inverse_state, row_seeds, col_seeds):
    row_blocks, block, col_blocks, _ = inverse_state.shape
    row_count, col_count = lax.axis_size("row"), lax.axis_size("col")
    halves = block // LANES
    lines = block * halves * col_blocks
    width = col_blocks * block
    local_cols = col_blocks % 4 == 0
    f32 = jnp.float32
    vmem = pl.BlockSpec(memory_space=pltpu.VMEM)
    smem = pl.BlockSpec(memory_space=pltpu.SMEM)
    params = functools.partial(pltpu.CompilerParams, vmem_limit_bytes=VMEM_BYTES)

    native = inverse_state.reshape(row_blocks, block, col_blocks, halves, LANES)
    native = native.transpose(0, 1, 3, 2, 4).reshape(row_blocks, lines, LANES)
    row, col = lax.axis_index("row"), lax.axis_index("col")
    row_step, col_step = row - (row_count - STEPS), col - (col_count - STEPS)
    flags = jnp.stack([
        col_step >= 0, col_step, row_step, jnp.logical_and(col_step >= 0, col_step == row_step),
    ]).astype(jnp.int32)
    row_scales = (seed_values(row_seeds) * root_half).reshape(2 * row_blocks, block).T
    col_scales = (seed_values(col_seeds) * root_half).reshape(2, width)

    column, pivot_rows = pl.pallas_call(
        functools.partial(extract_kernel, row_blocks, col_blocks, block),
        grid=(row_blocks,),
        in_specs=[pl.BlockSpec((None, lines, LANES), lambda a: (a, 0, 0))],
        out_specs=[
            pl.BlockSpec((1, block, block), lambda a: (a, 0, 0)),
            pl.BlockSpec((block, width), lambda a: (0, 0)),
        ],
        out_shape=[
            jax.ShapeDtypeStruct((row_blocks, block, block), f32),
            jax.ShapeDtypeStruct((block, width), f32),
        ],
        name="extract",
        compiler_params=params(),
    )(native)

    chunks, pieces = 2 * row_blocks, 4
    dma = pltpu.SemaphoreType.DMA
    panel, rows, pivot = pl.pallas_call(
        functools.partial(spread_kernel, chunks, pieces, col_count, row_count),
        in_specs=[vmem, vmem],
        out_specs=[vmem, vmem, vmem],
        out_shape=[
            jax.ShapeDtypeStruct((STEPS, row_blocks, block, block), f32),
            jax.ShapeDtypeStruct((STEPS, block, width), f32),
            jax.ShapeDtypeStruct((STEPS, STEPS, block, block), f32),
        ],
        scratch_shapes=[dma((chunks,))] * 4 + [dma((pieces,))] * 4 + [dma] * 6 + [dma((3,))],
        name="spread",
        compiler_params=params(collective_id=0, has_side_effects=True),
    )(column, pivot_rows)

    high, low = pl.pallas_call(
        functools.partial(solve_kernel, col_blocks, block, local_cols),
        in_specs=[smem, vmem, vmem, vmem],
        out_specs=[vmem, vmem],
        out_shape=[jax.ShapeDtypeStruct((STEPS * block, width), jnp.bfloat16)] * 2,
        name="solve",
        compiler_params=params(),
    )(flags, pivot, rows, col_scales)

    tile = block // 4
    whole = lambda i: (0, 0)
    out = pl.pallas_call(
        functools.partial(final_kernel, row_blocks, col_blocks, block, tile, local_cols),
        grid=(block // tile,),
        in_specs=[
            smem,
            pl.BlockSpec((row_blocks, lines // 4, LANES), lambda i: (0, i, 0)),
            pl.BlockSpec((STEPS, row_blocks, tile, block), lambda i: (0, 0, i, 0)),
            pl.BlockSpec((tile, 2 * row_blocks), lambda i: (i, 0)),
            pl.BlockSpec((2, width), whole),
            pl.BlockSpec((STEPS * block, width), whole),
            pl.BlockSpec((STEPS * block, width), whole),
        ],
        out_specs=pl.BlockSpec((row_blocks, lines // 4, LANES), lambda i: (0, i, 0)),
        out_shape=jax.ShapeDtypeStruct((row_blocks, lines, LANES), f32),
        scratch_shapes=[
            pltpu.VMEM((row_blocks * tile, STEPS * block), jnp.bfloat16),
            pltpu.VMEM((row_blocks * tile, STEPS * block), jnp.bfloat16),
            pltpu.VMEM((row_blocks * tile, width), f32),
        ],
        name="final",
        compiler_params=params(),
    )(flags, native, panel, row_scales, col_scales, high, low)
    out = out.reshape(row_blocks, block, halves, col_blocks, LANES).transpose(0, 1, 3, 2, 4)
    out = out.reshape(inverse_state.shape)
    if not local_cols:
        flat = out.reshape(row_blocks * block, col_blocks, block)
        out = col_butterfly(flat, col_seeds).reshape(inverse_state.shape)
    return out


def solution(mesh):
    placed = (P(None, "row", None, "col"), P(None, None, "row"), P(None, None, "col"))
    return jax.shard_map(
        per_device,
        mesh=mesh,
        in_specs=placed,
        out_specs=P(None, "row", None, "col"),
        check_vma=False,
    )
```

time: 535 us -> 133 us (0.25); the launches traced: 525 us -> 133 us
  local copies, waits for them, and re-layouts: 164 us -> 1.37 us
  waiting for transfers between devices: 159 us -> 0 us
  other arithmetic: 148 us -> 2.08 us
  Pallas kernels: 0 us -> 130 us
  matrix products: 37.3 us -> 0 us
  between operations: 16.8 us -> 0.01 us
    psum x4 -> x0, waiting for transfers between devices: 159 us -> none  [broadcast(): return lax.psum(jnp.where(mine, x, jnp.zeros_like(x)), axis)]
    pallas_call x0 -> x4, Pallas kernels: none -> 130 us  [the longest x1 81.9 us: per_device(): pl.pallas_call(functools.partial(spread_kernel, chunks, pieces, col_count...]
    another operation x21 -> x1, other arithmetic: 110 us -> 0.65 us  [per_device(): jnp.stack([col_step >= 0, col_step, row_step, jnp.logical_and(col_step >=...]
    scatter x4 -> x0, local copies, waits for them, and re-layouts: 97.2 us -> none  [the longest x2 91.6 us: pivot_pieces(): shifted = state.at[:, :, col_local, :].set(last_column)]
    dot_general x6 -> x0, matrix products: 29 us -> none  [the longest x1 11.3 us: per_device(): jnp.dot(left_moved, right_moved.reshape(block, col_blocks * block), preci...]
    reshape x2 -> x1, local copies, waits for them, and re-layouts: 23.1 us -> 0.77 us  [per_device(): (seed_values(row_seeds) * root_half).reshape(2 * row_blocks, block)]
    unnamed x18 -> x1, local copies, waits for them, and re-layouts: 19.4 us -> 0.6 us
    slice x5 -> x0, local copies, waits for them, and re-layouts: 12.4 us -> none  [the longest x2 12.4 us: pivot_pieces(): last_column = jnp.where(on_col, 0.0, state[:, :, col_local, :])]
  transfers between devices with their start and end apart: 4 -> 0, of which waited for: 4 -> 0; matrix products, arithmetic and copies ran while one was open for 17% -> 0% of each run, Pallas kernels for 0% -> 0%
where the time goes in v1:
time: 133 us
  Pallas kernels  130 us (98%)
  other arithmetic  2.08 us (2%)
  local copies, waits for them, and re-layouts  1.37 us (1%)
    pallas_call x1, Pallas kernels, per_device(): pl.pallas_call(functools.partial(spread_kernel, chunks, pieces, col_count...  81.9 us
    pallas_call x1, Pallas kernels, per_device(): pl.pallas_call(functools.partial(solve_kernel, col_blocks, block, local_c...  25.6 us
    pallas_call x1, Pallas kernels, per_device(): pl.pallas_call(functools.partial(final_kernel, row_blocks, col_blocks, bl...  14.4 us
    pallas_call x1, Pallas kernels, per_device(): pl.pallas_call(functools.partial(extract_kernel, row_blocks, col_blocks,...  7.63 us

profile of v1, /device:TPU:0, one launch (start us, length us, event | category | flops | bytes accessed | tf_op | source)
XLA Modules:
  0.0 133.0 jit_solution(8728509146492972541)
XLA Ops:
  0.0 0.7 pad_add_fusion.flags
  0.7 0.7 multiply_bitcast_fusion.1
  1.4 0.6 copy.10
  2.0 0.7 multiply_bitcast_fusion
  2.7 0.8 copy.8
  3.5 7.6 %extract.1 = (f32[8,256,256]{2,1,0:T(8,128)}, f32[256,1024]{1,0:T(8,128)}) custom-call(f32[8,2048,128]{2,1,0:T(8,128)} %bitcast.20), custom_call_target="tpu_custom_call" | custom-call | tf_op jit(solution)/shard_map/extract/pallas_call | solution.py:369
  11.1 81.9 %spread.1 = (f32[2,8,256,256]{3,2,1,0:T(8,128)}, f32[2,256,1024]{2,1,0:T(8,128)}, f32[2,2,256,256]{3,2,1,0:T(8,128)}) custom-call(f32[8,256,256]{2,1,0:T(8,128)} %get-tuple-element.12.c_ref, f32[256,1024]{1,0:T(8,128)} %get-tuple-element.13.r_ref), custom_call_target="tpu_custom_call" | custom-call | tf_op jit(solution)/shard_map/spread/pallas_call | solution.py:387
  93.0 25.6 %solve.1 = (bf16[512,1024]{1,0:T(8,128)(2,1)}, bf16[512,1024]{1,0:T(8,128)(2,1)}) custom-call(s32[4]{0:T(128)} %pad_add_fusion.flags, f32[2,2,256,256]{3,2,1,0:T(8,128)} %get-tuple-element.15.p_ref, f32[2,256,1024]{2,1,0:T(8,128)} %get-tuple-element.16.r_ref, f32[2,1024]{1,0:T(2,128)} %bitcast.23), custom_call_target="tpu_custom_call" | custom-call | tf_op jit(solution)/shard_map/solve/pallas_call | solution.py:401
  118.6 14.4 %final.1 = f32[8,2048,128]{2,1,0:T(8,128)} custom-call(s32[4]{0:T(128)} %pad_add_fusion.flags, f32[8,2048,128]{2,1,0:T(8,128)} %bitcast.21, f32[2,8,256,256]{3,2,1,0:T(8,128)} %get-tuple-element.14.c_ref, f32[256,16]{1,0:T(8,128)} %bitcast.22, f32[2,1024]{1,0:T(2,128)} %bitcast.24, bf16[512,1024]{1,0:T(8,128)(2,1)} %get-tuple-element.17.high_ref, ...), custom_call_target="tpu_custom_call" | custom-call | tf_op jit(solution)/shard_map/final/pallas_call | solution.py:412
